TPU v7x, 32 devices: a whole 2x2x4 slice. The times are simulated.
32 devices in a mesh: groups: 2 (over y), ctx: 8 (over z, x), head: 2 (over core).
Axes of the slice: x: 2, y: 2, z: 4, core: 2. Of those that a mesh axis runs over, the one named last changes fastest.
Arguments:
- query_latent: bfloat16 [16, 64, 576], P(('groups', 'ctx'), 'head'), parts along dimension 0, may hold values from -9 to 9
- latent_codes: bfloat16 [4096, 576], P(('groups', 'ctx')), parts along dimension 0, may hold values from -6 to 6
- latent_scales: float32 [4096, 9], P(('groups', 'ctx')), parts along dimension 0, may hold values from 0.5 to 2
- valid_lengths: int32 [16], P(('groups', 'ctx')), parts along dimension 0, may hold values from 1 to 256
- query_position: int32 [16], P('groups'), parts along dimension 0, may hold values from 0 to 2047
- value_up: bfloat16 [64, 512, 128], P('head'), may hold values from -1 to 1
- out_codes: bfloat16 [8192, 7168], P('head', 'ctx'), may hold values from -0.0625 to 0.0625
- out_scales: float32 [7168], P('ctx'), may hold values from 0.5 to 2
Outputs:
- attention: bfloat16 [16, 8192], P(('groups', 'ctx'), 'head'), parts along dimension 0
- projected: bfloat16 [16, 7168], P(('groups', 'head'), 'ctx'), parts along dimension 0
There are 2 independent parts, one for each index of `groups`. A program takes and returns all parts, laid end to end along the dimension named above; an argument that names none is the same for every part. Nothing has to cross between parts.
All inputs are finite; a program needn't handle non-finite values.
Results may differ from a plain program's by a relative error of at most 0.011.
Values may be sent and summed in bfloat16 or wider, within the bound.
A program may use at most 128 MiB of HBM per device.

v0:
```python
import functools

import jax
import jax.numpy as jnp
from jax import lax
from jax.experimental import pallas as pl
from jax.experimental.pallas import tpu as pltpu
from jax.sharding import PartitionSpec as P

LAT_NOPE = 512
ROPE = 64
QK_NOPE = 128
LANES = 128
MASKED = -1e30
MESH = pl.DeviceIdType.MESH


def shards(
    query_latent,
    latent_codes,
    latent_scales,
    valid_lengths,
    query_position,
    value_up,
    out_codes,
    out_scales,
):
    key_count, width = latent_codes.shape
    block_count = latent_scales.shape[1]
    latent = (
        (
            latent_codes.astype(jnp.float32).reshape(key_count, block_count, width // block_count)
            * latent_scales[:, :, None]
        )
        .reshape(key_count, width)
        .astype(jnp.bfloat16)
    )
    shard_index = lax.axis_index("ctx")
    local_slots = jnp.arange(key_count, dtype=jnp.int32)
    key_pos = shard_index * key_count + local_slots
    usable = local_slots < valid_lengths[0]
    softmax_scale = (QK_NOPE + ROPE) ** (-0.5)
    logits = (
        jnp.einsum(
            "qhc,kc->qhk",
            lax.all_gather(query_latent, "ctx", axis=0, tiled=True),
            latent,
            preferred_element_type=jnp.float32,
        )
        * softmax_scale
    )
    allowed = usable[None, :] & (key_pos[None, :] <= query_position[:, None])
    scores = jnp.where(allowed[:, None, :], logits, -jnp.inf)
    maxima = lax.pmax(jnp.max(scores, axis=2), "ctx")
    weights = jnp.exp(scores - maxima[:, :, None])
    totals = jnp.sum(weights, axis=2)
    latent_mix = jnp.einsum(
        "qhk,kd->qhd",
        weights.astype(jnp.bfloat16),
        latent[:, :LAT_NOPE],
        preferred_element_type=jnp.float32,
    ).astype(jnp.bfloat16)
    values = jnp.einsum("qhd,hdv->qhv", latent_mix, value_up, preferred_element_type=jnp.float32)
    queries, head_count, value_width = values.shape
    numerators = values.reshape(queries, head_count * value_width)
    own_rows = query_latent.shape[0]
    numer_sum, denom_sum = lax.psum((numerators, totals), "ctx")
    attn_all = (
        (numer_sum.reshape(queries, head_count, value_width) / denom_sum[:, :, None])
        .reshape(queries, head_count * value_width)
        .astype(jnp.bfloat16)
    )
    attn_home = lax.dynamic_slice_in_dim(attn_all, shard_index * own_rows, own_rows, 0)
    summed = lax.psum_scatter(
        jnp.dot(attn_all, out_codes, preferred_element_type=jnp.float32),
        "head",
        scatter_dimension=0,
        tiled=True,
    )
    projected = (summed * out_scales[None, :]).astype(jnp.bfloat16)
    return (attn_home, projected)


def fused(
    n,
    heads,
    valid_ref,
    qpos_ref,
    query_hbm,
    codes_hbm,
    scales_hbm,
    up_hbm,
    out_hbm,
    attn_ref,
    proj_ref,
    q_all,
    codes,
    scales,
    up,
    outw,
    latent,
    mix,
    stat_m,
    stat_l,
    num_send,
    num_recv,
    st_send,
    st_recv,
    att_all,
    part,
    part_recv,
    in_sem,
    up_sem,
    out_sem,
    q_send,
    q_recv,
    num_ssem,
    num_rsem,
    st_ssem,
    st_rsem,
    att_ssem,
    att_rsem,
    part_ssem,
    part_rsem,
):
    me = lax.axis_index("ctx")
    hd = lax.axis_index("head")
    side = lax.rem(me, 2)
    partner = me + 1 - 2 * side
    half = n // 2
    tokens, head_count, width = q_all.shape
    keys = codes.shape[1]
    nope = mix.shape[0] * LANES
    vhead = up.shape[2]
    per = head_count // n
    cols = per * vhead

    def at(k):
        return lax.rem(me + k + n, n)

    barrier = pltpu.get_barrier_semaphore()
    for k in range(1, n):
        pl.semaphore_signal(barrier, inc=1, device_id={"ctx": at(k)}, device_id_type=MESH)
    for k in range(1, heads):
        pl.semaphore_signal(
            barrier, inc=1, device_id={"head": lax.rem(hd + k, heads)}, device_id_type=MESH
        )

    own_q = pltpu.make_async_copy(query_hbm.at[0], q_all.at[me], in_sem.at[0])
    own_q.start()
    codes_in = pltpu.make_async_copy(codes_hbm, codes, in_sem.at[1])
    codes_in.start()
    scales_in = pltpu.make_async_copy(scales_hbm, scales, in_sem.at[2])
    scales_in.start()
    up_in = []
    for g in range(n):
        rows = pl.ds(g * per, per)
        up_in.append(pltpu.make_async_copy(up_hbm.at[rows], up.at[rows], up_sem.at[g]))
        up_in[-1].start()
    out_in = []
    for g in range(n):
        rows = pl.ds(g * cols, cols)
        out_in.append(pltpu.make_async_copy(out_hbm.at[rows], outw.at[rows], out_sem.at[g]))
        out_in[-1].start()

    own_q.wait()
    pl.semaphore_wait(barrier, n - 1 + heads - 1)

    def send_q(token, target, index):
        copy = pltpu.make_async_remote_copy(
            src_ref=q_all.at[token],
            dst_ref=q_all.at[token],
            send_sem=q_send.at[index],
            recv_sem=q_recv.at[index],
            device_id={"ctx": target},
            device_id_type=MESH,
        )
        copy.start()
        return copy

    sent = [send_q(me, partner, half)]
    direct = [send_q(me, at(2 * k), k) for k in range(1, half)]

    codes_in.wait()
    scales_in.wait()
    block = width // scales.shape[0]
    for b in range(scales.shape[0]):
        rows = slice(b * block, (b + 1) * block)
        latent[rows, :] = (codes[rows, :].astype(jnp.float32) * scales[b : b + 1, :]).astype(jnp.bfloat16)

    for k in range(1, half):
        direct[k - 1].wait_recv()
        sent.append(send_q(at(-2 * k), partner, half + k))
    for copy in sent:
        copy.wait_recv()

    softmax_scale = (QK_NOPE + ROPE) ** (-0.5)
    logits = (
        jnp.dot(
            q_all[...].reshape(tokens * head_count, width),
            latent[...],
            preferred_element_type=jnp.float32,
        )
        * softmax_scale
    )
    slot = lax.broadcasted_iota(jnp.int32, (head_count, keys), 1)
    weights = []
    for t in range(tokens):
        limit = jnp.minimum(valid_ref[0], qpos_ref[t] - me * keys + 1)
        allowed = slot < limit
        rows = slice(t * head_count, (t + 1) * head_count)
        scores = jnp.where(allowed, logits[rows], MASKED)
        top = jnp.max(scores, axis=1, keepdims=True)
        weight = jnp.where(allowed, jnp.exp(scores - top), 0.0)
        stat_m[rows, :] = jnp.broadcast_to(top, (head_count, LANES))
        stat_l[rows, :] = jnp.broadcast_to(jnp.sum(weight, axis=1, keepdims=True), (head_count, LANES))
        weights.append(weight.astype(jnp.bfloat16))
    mixed_all = lax.dot_general(
        jnp.concatenate(weights, axis=0),
        latent[:nope, :],
        (((1,), (1,)), ((), ())),
        preferred_element_type=jnp.float32,
    )
    for c in range(mix.shape[0]):
        mix[c] = mixed_all[:, c * LANES : (c + 1) * LANES]

    tile_lane = lax.broadcasted_iota(jnp.int32, (tokens, LANES), 1)
    for g in range(n):
        up_in[g].wait()
        stat = jnp.zeros((tokens, LANES), jnp.float32)
        for j in range(per):
            h = g * per + j
            rows = pl.ds(h, tokens, stride=head_count)
            mixed = jnp.concatenate(
                [mix[c, rows, :] for c in range(mix.shape[0])], axis=1
            ).astype(jnp.bfloat16)
            num_send[g, :, j * vhead : (j + 1) * vhead] = jnp.dot(
                mixed, up[h], preferred_element_type=jnp.float32
            ).astype(jnp.bfloat16)
            stat = jnp.where(tile_lane == j, stat_m[rows, :], stat)
            stat = jnp.where(tile_lane == per + j, stat_l[rows, :], stat)
        st_send[g] = stat

    moved = []
    for k in range(1, n):
        target = at(k)
        for src, dst, ssem, rsem in (
            (st_send, st_recv, st_ssem, st_rsem),
            (num_send, num_recv, num_ssem, num_rsem),
        ):
            copy = pltpu.make_async_remote_copy(
                src_ref=src.at[target],
                dst_ref=dst.at[k],
                send_sem=ssem.at[k],
                recv_sem=rsem.at[k],
                device_id={"ctx": target},
                device_id_type=MESH,
            )
            copy.start()
            moved.append(copy)
    for copy in direct + sent:
        copy.wait_send()
    for copy in moved:
        copy.wait_recv()

    stats = [st_send[me]] + [st_recv[k] for k in range(1, n)]
    nums = [num_send[me]] + [num_recv[k] for k in range(1, n)]
    top = functools.reduce(jnp.maximum, stats)
    factors = [jnp.exp(s - top) for s in stats]
    pieces = []
    for j in range(per):
        total = jnp.zeros((tokens, 1), jnp.float32)
        value = jnp.zeros((tokens, vhead), jnp.float32)
        for s, f, v in zip(stats, factors, nums):
            factor = f[:, j : j + 1]
            total += factor * s[:, per + j : per + j + 1]
            value += factor * v[:, j * vhead : (j + 1) * vhead].astype(jnp.float32)
        pieces.append((value / total).astype(jnp.bfloat16))
    att_all[me] = jnp.concatenate(pieces, axis=1)

    shared = []
    for k in range(1, n):
        copy = pltpu.make_async_remote_copy(
            src_ref=att_all.at[me],
            dst_ref=att_all.at[me],
            send_sem=att_ssem.at[k],
            recv_sem=att_rsem.at[k],
            device_id={"ctx": at(k)},
            device_id_type=MESH,
        )
        copy.start()
        shared.append(copy)
    for copy in moved:
        copy.wait_send()
    for copy in out_in:
        copy.wait()
    columns = outw.shape[1]
    acc = jnp.zeros((tokens, columns), jnp.float32)
    for k in range(n):
        if k:
            shared[k - 1].wait_recv()
        g = at(-k)
        acc += jnp.dot(
            att_all[g],
            outw[pl.ds(pl.multiple_of(g * cols, cols), cols), :],
            preferred_element_type=jnp.float32,
        )
    rows = tokens // heads
    for i in range(heads):
        part[i] = acc[i * rows : (i + 1) * rows]
    swapped = []
    for k in range(1, heads):
        other = lax.rem(hd + k, heads)
        copy = pltpu.make_async_remote_copy(
            src_ref=part.at[other],
            dst_ref=part_recv.at[k],
            send_sem=part_ssem.at[k],
            recv_sem=part_rsem.at[k],
            device_id={"head": other},
            device_id_type=MESH,
        )
        copy.start()
        swapped.append(copy)
    row = lax.broadcasted_iota(jnp.int32, (tokens, cols), 0)
    for g in range(n):
        attn_ref[:, g * cols : (g + 1) * cols] = jnp.sum(
            jnp.where(row == me, att_all[g].astype(jnp.float32), 0.0), axis=0, keepdims=True
        )
    summed = part[hd]
    for k in range(1, heads):
        swapped[k - 1].wait_recv()
        summed += part_recv[k]
    proj_ref[...] = summed
    for copy in shared + swapped:
        copy.wait_send()


def block(n, heads, *args):
    query, codes, scales, valid, qpos, up, outw, out_scales = args
    own, head_count, width = query.shape
    tokens = own * n
    fits = own == 1 and n % 2 == 0 and head_count % n == 0 and tokens % (4 * heads) == 0
    if not fits:
        return shards(*args)
    keys = codes.shape[0]
    vhead = up.shape[2]
    per = head_count // n
    cols = per * vhead
    columns = outw.shape[1]
    anywhere = pl.BlockSpec(memory_space=pl.ANY)
    vmem = pl.BlockSpec(memory_space=pltpu.VMEM)
    smem = pl.BlockSpec(memory_space=pltpu.SMEM)
    dma = pltpu.SemaphoreType.DMA
    attention, summed = pl.pallas_call(
        functools.partial(fused, n, heads),
        out_shape=(
            jax.ShapeDtypeStruct((own, head_count * vhead), jnp.float32),
            jax.ShapeDtypeStruct((tokens // heads, columns), jnp.float32),
        ),
        in_specs=[smem, smem] + [anywhere] * 5,
        out_specs=(vmem, vmem),
        scratch_shapes=[
            pltpu.VMEM((tokens, head_count, width), jnp.bfloat16),
            pltpu.VMEM((width, keys), jnp.bfloat16),
            pltpu.VMEM(scales.shape[::-1], jnp.float32),
            pltpu.VMEM(up.shape, jnp.bfloat16),
            pltpu.VMEM(outw.shape, jnp.bfloat16),
            pltpu.VMEM((width, keys), jnp.bfloat16),
            pltpu.VMEM((LAT_NOPE // LANES, tokens * head_count, LANES), jnp.float32),
            pltpu.VMEM((tokens * head_count, LANES), jnp.float32),
            pltpu.VMEM((tokens * head_count, LANES), jnp.float32),
            pltpu.VMEM((n, tokens, cols), jnp.bfloat16),
            pltpu.VMEM((n, tokens, cols), jnp.bfloat16),
            pltpu.VMEM((n, tokens, LANES), jnp.float32),
            pltpu.VMEM((n, tokens, LANES), jnp.float32),
            pltpu.VMEM((n, tokens, cols), jnp.bfloat16),
            pltpu.VMEM((heads, tokens // heads, columns), jnp.float32),
            pltpu.VMEM((heads, tokens // heads, columns), jnp.float32),
            dma((3,)),
            dma((n,)),
            dma((n,)),
            dma((n,)),
            dma((n,)),
            dma((n,)),
            dma((n,)),
            dma((n,)),
            dma((n,)),
            dma((n,)),
            dma((n,)),
            dma((heads,)),
            dma((heads,)),
        ],
        compiler_params=pltpu.CompilerParams(collective_id=0, has_side_effects=True),
        name="mla_block",
    )(valid, qpos, query, codes.T, scales.T, up, outw)
    projected = (summed * out_scales[None, :]).astype(jnp.bfloat16)
    return attention.astype(jnp.bfloat16), projected


def solution(mesh):
    ctx, heads = mesh.shape["ctx"], mesh.shape["head"]
    return jax.shard_map(
        functools.partial(block, ctx, heads),
        mesh=mesh,
        in_specs=(
            P(("groups", "ctx"), "head", None),
            P(("groups", "ctx"), None),
            P(("groups", "ctx"), None),
            P(("groups", "ctx")),
            P("groups"),
            P("head", None, None),
            P("head", "ctx"),
            P("ctx"),
        ),
        out_specs=(P(("groups", "ctx"), "head"), P(("groups", "head"), "ctx")),
        check_vma=False,
    )
```

profile of v0, /device:TPU:0, one launch (start us, length us, event | category | flops | bytes accessed | tf_op | source)
XLA Modules:
  0.0 35.0 jit_solution(7563698036203872743)
XLA Ops:
  0.6 0.0 copy-start
  1.3 31.1 %mla_block.1 = (f32[1,4096]{1,0:T(1,128)}, f32[4,896]{1,0:T(4,128)}) custom-call(s32[1]{0:T(128)S(6)} %copy.10.valid_ref, s32[8]{0:T(128)} %qpos_ref.1, bf16[1,32,576]{2,1,0:T(8,128)(2,1)} %query_hbm.1, bf16[576,256]{1,0:T(8,128)(2,1)} %bitcast.2, f32[9,256]{1,0:T(8,128)} %bitcast.3, bf16[32,512,128]{2,1,0:T(8,128)(2,1)} %up_hbm.1, bf16[4096,896]{1,0:T(8,128)(2,1)} %out_hbm.1), custom_call_target="tpu_custom_call" | custom-call | tf_op jit(solution)/shard_map/mla_block/pallas_call | solution.py:354
  32.4 1.3 %convert_element_type.6 = bf16[1,4096]{1,0:T(2,128)(2,1)} convert(f32[1,4096]{1,0:T(1,128)} %get-tuple-element.4) | non-fusion elementwise | flops 4096 | bytes 24576 | tf_op jit(solution)/shard_map/convert_element_type | solution.py:397
  33.7 0.0 copy-done
  33.7 1.3 %multiply_convert_fusion = bf16[4,896]{1,0:T(4,128)(2,1)} fusion(f32[4,896]{1,0:T(4,128)} %get-tuple-element.5, f32[896]{0:T(1024)S(1)} %copy-done), kind=kLoop, calls=%fused_computation | loop fusion | flops 7168 | bytes 25088 | tf_op jit(solution)/shard_map/convert_element_type | solution.py:396
Async XLA Ops:
  0.6 33.1 %copy-start = (f32[896]{0:T(1024)S(1)}, f32[896]{0:T(1024)}, u32[]{:S(2)}) copy-start(f32[896]{0:T(1024)} %param.15) | copy-start | bytes 10756
where the time goes:
time: 35.4 us; the launch traced here: 35 us
  Pallas kernels  31.1 us (88%)
  other arithmetic  2.65 us (7%)
  between operations  1.31 us (4%)
    pallas_call x1, Pallas kernels, block(): pl.pallas_call(functools.partial(fused, n, heads), out_shape=(jax.ShapeDt...  31.1 us
    convert_element_type x1, other arithmetic, block(): return (attention.astype(jnp.bfloat16), projected)  1.34 us
    convert_element_type x1, other arithmetic, block(): projected = (summed * out_scales[None, :]).astype(jnp.bfloat16)  1.31 us

commit v1 on v0

v1 whole, which is shorter than its diff:
```python
import functools
import math

import jax
import jax.numpy as jnp
from jax import lax
from jax.experimental import pallas as pl
from jax.experimental.pallas import tpu as pltpu
from jax.sharding import PartitionSpec as P

LAT_NOPE = 512
ROPE = 64
QK_NOPE = 128
LANES = 128
MASKED = -1e30
MESH = pl.DeviceIdType.MESH


def shards(
    query_latent,
    latent_codes,
    latent_scales,
    valid_lengths,
    query_position,
    value_up,
    out_codes,
    out_scales,
):
    key_count, width = latent_codes.shape
    block_count = latent_scales.shape[1]
    latent = (
        (
            latent_codes.astype(jnp.float32).reshape(key_count, block_count, width // block_count)
            * latent_scales[:, :, None]
        )
        .reshape(key_count, width)
        .astype(jnp.bfloat16)
    )
    shard_index = lax.axis_index("ctx")
    local_slots = jnp.arange(key_count, dtype=jnp.int32)
    key_pos = shard_index * key_count + local_slots
    usable = local_slots < valid_lengths[0]
    softmax_scale = (QK_NOPE + ROPE) ** (-0.5)
    logits = (
        jnp.einsum(
            "qhc,kc->qhk",
            lax.all_gather(query_latent, "ctx", axis=0, tiled=True),
            latent,
            preferred_element_type=jnp.float32,
        )
        * softmax_scale
    )
    allowed = usable[None, :] & (key_pos[None, :] <= query_position[:, None])
    scores = jnp.where(allowed[:, None, :], logits, -jnp.inf)
    maxima = lax.pmax(jnp.max(scores, axis=2), "ctx")
    weights = jnp.exp(scores - maxima[:, :, None])
    totals = jnp.sum(weights, axis=2)
    latent_mix = jnp.einsum(
        "qhk,kd->qhd",
        weights.astype(jnp.bfloat16),
        latent[:, :LAT_NOPE],
        preferred_element_type=jnp.float32,
    ).astype(jnp.bfloat16)
    values = jnp.einsum("qhd,hdv->qhv", latent_mix, value_up, preferred_element_type=jnp.float32)
    queries, head_count, value_width = values.shape
    numerators = values.reshape(queries, head_count * value_width)
    own_rows = query_latent.shape[0]
    numer_sum, denom_sum = lax.psum((numerators, totals), "ctx")
    attn_all = (
        (numer_sum.reshape(queries, head_count, value_width) / denom_sum[:, :, None])
        .reshape(queries, head_count * value_width)
        .astype(jnp.bfloat16)
    )
    attn_home = lax.dynamic_slice_in_dim(attn_all, shard_index * own_rows, own_rows, 0)
    summed = lax.psum_scatter(
        jnp.dot(attn_all, out_codes, preferred_element_type=jnp.float32),
        "head",
        scatter_dimension=0,
        tiled=True,
    )
    projected = (summed * out_scales[None, :]).astype(jnp.bfloat16)
    return (attn_home, projected)


def flip(index, mask):
    bit, result = 1, index
    while bit <= mask:
        if mask & bit:
            result = result + bit - 2 * bit * lax.rem(index // bit, 2)
        bit *= 2
    return result


def fused(
    n,
    heads,
    valid_hbm,
    qpos_hbm,
    query_hbm,
    codes_hbm,
    scales_hbm,
    up_hbm,
    out_hbm,
    attn_ref,
    proj_ref,
    valid,
    qpos,
    near_valid,
    q_all,
    codes,
    near_codes,
    scales,
    near_scales,
    up,
    outw,
    latent,
    near_latent,
    mix,
    stat_m,
    stat_l,
    num_send,
    num_recv,
    st_send,
    st_recv,
    att_all,
    part,
    part_recv,
    ready,
    in_sem,
    up_sem,
    out_sem,
    q_ssem,
    q_rsem,
    near_ssem,
    near_rsem,
    half_ssem,
    half_rsem,
    num_ssem,
    num_rsem,
    st_ssem,
    st_rsem,
    att_ssem,
    att_rsem,
    part_ssem,
    part_rsem,
):
    me = lax.axis_index("ctx")
    hd = lax.axis_index("head")
    other = 1 - hd
    row, column = me // 2, lax.rem(me, 2)
    rows = n // 2
    head_count, width = q_all.shape[1:]
    pieces, piece, keys = codes.shape
    each = pieces // heads
    nope = mix.shape[0] * LANES
    vhead = up.shape[2]
    twin = head_count // 2
    per = twin // rows
    lines = 2 * rows

    barrier = pltpu.get_barrier_semaphore()
    for k in range(n - 1, 0, -1):
        later = flip(me, k)

        @pl.when(later > me)
        def _():
            pl.semaphore_signal(barrier, inc=1, device_id={"ctx": later}, device_id_type=MESH)

    pl.semaphore_signal(barrier, inc=1, device_id={"head": other}, device_id_type=MESH)

    loads = [
        pltpu.make_async_copy(codes_hbm, codes, in_sem.at[0]),
        pltpu.make_async_copy(scales_hbm, scales, in_sem.at[1]),
        pltpu.make_async_copy(query_hbm.at[0], q_all.at[row], in_sem.at[2]),
        pltpu.make_async_copy(valid_hbm, valid, in_sem.at[3]),
        pltpu.make_async_copy(qpos_hbm, qpos, in_sem.at[4]),
    ]
    for copy in loads:
        copy.start()

    pl.semaphore_wait(barrier, me + heads - 1)

    for k in range(1, n):
        earlier = flip(me, k)

        @pl.when(earlier < me)
        def _():
            pl.semaphore_signal(ready.at[k], inc=1, device_id={"ctx": earlier}, device_id_type=MESH)

    def admit(k):
        @pl.when(flip(me, k) > me)
        def _():
            pl.semaphore_wait(ready.at[k], 1)

    def remote(src, dst, ssem, rsem, **device):
        copy = pltpu.make_async_remote_copy(
            src_ref=src,
            dst_ref=dst,
            send_sem=ssem,
            recv_sem=rsem,
            device_id=device,
            device_id_type=MESH,
        )
        copy.start()
        return copy

    admit(1)
    partner = flip(me, 1)
    near = [
        remote(
            codes_hbm.at[hd * each + i],
            near_codes.at[hd * each + i],
            near_ssem.at[i],
            near_rsem.at[i],
            ctx=partner,
        )
        for i in range(each)
    ]
    near.append(remote(scales_hbm, near_scales, near_ssem.at[each], near_rsem.at[each], ctx=partner))
    near.append(remote(valid_hbm, near_valid, near_ssem.at[each + 1], near_rsem.at[each + 1], ctx=partner))

    up_in = []
    for g in range(2):
        part_of = pl.ds(g * twin, twin)
        up_in.append(pltpu.make_async_copy(up_hbm.at[part_of], up.at[part_of], up_sem.at[g]))
        up_in[-1].start()

    queries = []
    for k in range(1, rows):
        admit(2 * k)
        queries.append(
            remote(query_hbm.at[0], q_all.at[row], q_ssem.at[k], q_rsem.at[k], ctx=flip(me, 2 * k))
        )

    out_in = []
    half = outw.shape[0] // 2
    for g in range(2):
        part_of = pl.ds(g * half, half)
        out_in.append(pltpu.make_async_copy(out_hbm.at[part_of], outw.at[part_of], out_sem.at[g]))
        out_in[-1].start()

    block = width // scales.shape[0]

    def scale_latent(source, factors, target):
        unit = math.gcd(piece, block)
        for p in range(pieces):
            for r in range(0, piece, unit):
                at = p * piece + r
                b = at // block
                target[at : at + unit, :] = (
                    source[p, r : r + unit, :].astype(jnp.float32) * factors[b : b + 1, :]
                ).astype(jnp.bfloat16)

    for copy in loads:
        copy.wait()
    scale_latent(codes, scales, latent)

    relayed = []
    for i in range(each):
        near[i].wait_recv()
        relayed.append(
            remote(
                near_codes.at[hd * each + i],
                near_codes.at[hd * each + i],
                half_ssem.at[i],
                half_rsem.at[i],
                head=other,
            )
        )
    for copy in near[each:]:
        copy.wait_recv()
    for copy in queries:
        copy.wait_recv()
    for copy in relayed:
        copy.wait_recv()
    scale_latent(near_codes, near_scales, near_latent)

    softmax_scale = (QK_NOPE + ROPE) ** (-0.5)
    query = q_all[...].reshape(rows * head_count, width)
    own_logits = jnp.dot(query, latent[...], preferred_element_type=jnp.float32) * softmax_scale
    near_logits = jnp.dot(query, near_latent[...], preferred_element_type=jnp.float32) * softmax_scale
    slot = lax.broadcasted_iota(jnp.int32, (head_count, keys), 1)
    own_weights, near_weights = [], []
    for t in range(rows):
        position = qpos[2 * t + column]
        own_allowed = slot < jnp.minimum(valid[0], position - me * keys + 1)
        near_allowed = slot < jnp.minimum(near_valid[0], position - partner * keys + 1)
        of = slice(t * head_count, (t + 1) * head_count)
        own_scores = jnp.where(own_allowed, own_logits[of], MASKED)
        near_scores = jnp.where(near_allowed, near_logits[of], MASKED)
        top = jnp.max(jnp.maximum(own_scores, near_scores), axis=1, keepdims=True)
        own_weight = jnp.where(own_allowed, jnp.exp(own_scores - top), 0.0)
        near_weight = jnp.where(near_allowed, jnp.exp(near_scores - top), 0.0)
        stat_m[of, :] = jnp.broadcast_to(top, (head_count, LANES))
        stat_l[of, :] = jnp.broadcast_to(
            jnp.sum(own_weight + near_weight, axis=1, keepdims=True), (head_count, LANES)
        )
        own_weights.append(own_weight.astype(jnp.bfloat16))
        near_weights.append(near_weight.astype(jnp.bfloat16))
    transposed = (((1,), (1,)), ((), ()))
    mixed_all = lax.dot_general(
        jnp.concatenate(own_weights, axis=0),
        latent[:nope, :],
        transposed,
        preferred_element_type=jnp.float32,
    ) + lax.dot_general(
        jnp.concatenate(near_weights, axis=0),
        near_latent[:nope, :],
        transposed,
        preferred_element_type=jnp.float32,
    )
    for c in range(mix.shape[0]):
        mix[c] = mixed_all[:, c * LANES : (c + 1) * LANES]

    tile_lane = lax.broadcasted_iota(jnp.int32, (lines, LANES), 1)
    even = lax.rem(lax.broadcasted_iota(jnp.int32, (lines, LANES), 0), 2) == 0
    moved = []
    for k in range(rows - 1, -1, -1):
        group = flip(row, k)
        stat = jnp.zeros((lines, LANES), jnp.float32)
        for j in range(per):
            of = pl.ds(group * per + j, lines, stride=twin)
            stat = jnp.where(tile_lane == j, stat_m[of, :], stat)
            stat = jnp.where(tile_lane == per + j, stat_l[of, :], stat)
        st_send[k] = stat
        if k:
            moved.append(
                remote(st_send.at[k], st_recv.at[k], st_ssem.at[k], st_rsem.at[k], ctx=flip(me, 2 * k))
            )
    for copy in up_in:
        copy.wait()
    for k in range(rows - 1, -1, -1):
        group = flip(row, k)
        for j in range(per):
            h = group * per + j
            of = pl.ds(h, lines, stride=twin)
            mixed = jnp.concatenate(
                [mix[c, of, :] for c in range(mix.shape[0])], axis=1
            ).astype(jnp.bfloat16)
            num_send[k, j] = jnp.where(
                even,
                jnp.dot(mixed, up[h], preferred_element_type=jnp.float32),
                jnp.dot(mixed, up[h + twin], preferred_element_type=jnp.float32),
            ).astype(jnp.bfloat16)
        if k:
            moved.append(
                remote(num_send.at[k], num_recv.at[k], num_ssem.at[k], num_rsem.at[k], ctx=flip(me, 2 * k))
            )
    for copy in moved:
        copy.wait_recv()

    stats = [st_send[0]] + [st_recv[k] for k in range(1, rows)]
    top = functools.reduce(jnp.maximum, stats)
    factors = [jnp.exp(s - top) for s in stats]
    for j in range(per):
        total = jnp.zeros((lines, 1), jnp.float32)
        value = jnp.zeros((lines, vhead), jnp.float32)
        for k, (s, f) in enumerate(zip(stats, factors)):
            factor = f[:, j : j + 1]
            total += factor * s[:, per + j : per + j + 1]
            value += factor * (num_recv if k else num_send)[k, j].astype(jnp.float32)
        att_all[row, column, j] = (value / total).astype(jnp.bfloat16)

    shared = {}
    for k in range(n - 1, 0, -1):
        if k % 2 and k > 1:
            admit(k)
        shared[k] = remote(
            att_all.at[row, column],
            att_all.at[row, column],
            att_ssem.at[k],
            att_rsem.at[k],
            ctx=flip(me, k),
        )
    for copy in near + queries + relayed + moved:
        copy.wait_send()
    for copy in out_in:
        copy.wait()
    columns = outw.shape[1]
    acc = jnp.zeros((2 * lines, columns), jnp.float32)
    both = lax.rem(lax.broadcasted_iota(jnp.int32, (2 * lines, LANES), 0), 2) == 0
    own_line = lax.broadcasted_iota(jnp.int32, (lines, LANES), 0)

    def keep(group):
        for j in range(per):
            tile = att_all[group, column, j].astype(jnp.float32)
            for p in range(2):
                at = pl.multiple_of((p * twin + group * per + j) * vhead, vhead)
                attn_ref[:, pl.ds(at, vhead)] = jnp.sum(
                    jnp.where(own_line == 2 * row + p, tile, 0.0), axis=0, keepdims=True
                )

    for k in range(rows):
        group = flip(row, k)
        if k:
            shared[2 * k].wait_recv()
        shared[2 * k + 1].wait_recv()
        evens, odds = [], []
        for j in range(per):
            tile = jnp.concatenate(
                [att_all[group, c, j].astype(jnp.float32) for c in range(2)], axis=0
            )
            evens.append(jnp.where(both, tile, 0.0).astype(jnp.bfloat16))
            odds.append(jnp.where(both, 0.0, tile).astype(jnp.bfloat16))
        for p, side in enumerate((evens, odds)):
            at = pl.multiple_of((p * twin + group * per) * vhead, per * vhead)
            acc += jnp.dot(
                jnp.concatenate(side, axis=1),
                outw[pl.ds(at, per * vhead), :],
                preferred_element_type=jnp.float32,
            )
        if k < rows - 1:
            keep(group)
    share = n // heads
    for i in range(heads):
        lots = []
        for token in range(i * share, (i + 1) * share):
            at = token % 2 * lines + token // 2 * 2
            lots.append(acc[at : at + 1] + acc[at + 1 : at + 2])
        part[i] = jnp.concatenate(lots, axis=0)
    swap = remote(part.at[other], part_recv, part_ssem.at[0], part_rsem.at[0], head=other)
    keep(flip(row, rows - 1))
    swap.wait_recv()
    proj_ref[...] = part[hd] + part_recv[...]
    for k in range(n - 1, 0, -1):
        shared[k].wait_send()
    swap.wait_send()


def finish(attn_ref, summed_ref, scales_ref, attn_out, proj_out):
    attn_out[...] = attn_ref[...].astype(jnp.bfloat16)
    proj_out[...] = (summed_ref[...] * scales_ref[...].reshape(1, -1)).astype(jnp.bfloat16)


def block(n, heads, *args):
    query, codes, scales, valid, qpos, up, outw, out_scales = args
    own, head_count, width = query.shape
    keys, blocks = scales.shape
    split = 3 * heads
    fits = own == 1 and heads == 2 and n >= 4 and n & (n - 1) == 0 and head_count % n == 0
    fits = fits and width % (split * 16) == 0
    if not fits:
        return shards(*args)
    vhead = up.shape[2]
    rows, lines = n // 2, n
    per = head_count // n
    columns = outw.shape[1]
    anywhere = pl.BlockSpec(memory_space=pltpu.HBM)
    vmem = pl.BlockSpec(memory_space=pltpu.VMEM)
    dma = pltpu.SemaphoreType.DMA
    attention, summed = pl.pallas_call(
        functools.partial(fused, n, heads),
        out_shape=(
            jax.ShapeDtypeStruct((own, head_count * vhead), jnp.float32),
            jax.ShapeDtypeStruct((n // heads, columns), jnp.float32),
        ),
        in_specs=[anywhere] * 7,
        out_specs=(vmem, vmem),
        scratch_shapes=[
            pltpu.SMEM(valid.shape, jnp.int32),
            pltpu.SMEM(qpos.shape, jnp.int32),
            pltpu.SMEM(valid.shape, jnp.int32),
            pltpu.VMEM((rows, head_count, width), jnp.bfloat16),
            pltpu.VMEM((split, width // split, keys), jnp.bfloat16),
            pltpu.VMEM((split, width // split, keys), jnp.bfloat16),
            pltpu.VMEM((blocks, keys), jnp.float32),
            pltpu.VMEM((blocks, keys), jnp.float32),
            pltpu.VMEM(up.shape, jnp.bfloat16),
            pltpu.VMEM(outw.shape, jnp.bfloat16),
            pltpu.VMEM((width, keys), jnp.bfloat16),
            pltpu.VMEM((width, keys), jnp.bfloat16),
            pltpu.VMEM((LAT_NOPE // LANES, rows * head_count, LANES), jnp.float32),
            pltpu.VMEM((rows * head_count, LANES), jnp.float32),
            pltpu.VMEM((rows * head_count, LANES), jnp.float32),
            pltpu.VMEM((rows, per, lines, vhead), jnp.bfloat16),
            pltpu.VMEM((rows, per, lines, vhead), jnp.bfloat16),
            pltpu.VMEM((rows, lines, LANES), jnp.float32),
            pltpu.VMEM((rows, lines, LANES), jnp.float32),
            pltpu.VMEM((rows, 2, per, lines, vhead), jnp.bfloat16),
            pltpu.VMEM((heads, n // heads, columns), jnp.float32),
            pltpu.VMEM((n // heads, columns), jnp.float32),
            pltpu.SemaphoreType.REGULAR((n,)),
            dma((5,)),
            dma((2,)),
            dma((2,)),
            dma((rows,)),
            dma((rows,)),
            dma((split // heads + 2,)),
            dma((split // heads + 2,)),
            dma((split // heads,)),
            dma((split // heads,)),
            dma((rows,)),
            dma((rows,)),
            dma((rows,)),
            dma((rows,)),
            dma((n,)),
            dma((n,)),
            dma((1,)),
            dma((1,)),
        ],
        compiler_params=pltpu.CompilerParams(
            collective_id=0, has_side_effects=True
        ),
        name="mla_block",
    )(
        valid,
        qpos,
        query,
        codes.T.reshape(split, width // split, keys),
        scales.T,
        up,
        outw,
    )
    return pl.pallas_call(
        finish,
        out_shape=(
            jax.ShapeDtypeStruct((own, head_count * vhead), jnp.bfloat16),
            jax.ShapeDtypeStruct((n // heads, columns), jnp.bfloat16),
        ),
        in_specs=[vmem] * 3,
        out_specs=(vmem, vmem),
        name="finish",
    )(attention, summed, out_scales)


def solution(mesh):
    ctx, heads = mesh.shape["ctx"], mesh.shape["head"]
    return jax.shard_map(
        functools.partial(block, ctx, heads),
        mesh=mesh,
        in_specs=(
            P(("groups", "ctx"), "head", None),
            P(("groups", "ctx"), None),
            P(("groups", "ctx"), None),
            P(("groups", "ctx")),
            P("groups"),
            P("head", None, None),
            P("head", "ctx"),
            P("ctx"),
        ),
        out_specs=(P(("groups", "ctx"), "head"), P(("groups", "head"), "ctx")),
        check_vma=False,
    )
```

time: 35.4 us -> 24.9 us (0.70)
  Pallas kernels: 31.1 us -> 23.4 us
  other arithmetic: 2.65 us -> 0 us
    pallas_call x1, Pallas kernels: 31.1 us -> 22 us  [block(): pl.pallas_call(functools.partial(fused, n, heads), out_shape=(jax.ShapeDt...]
    convert_element_type x2 -> x0, other arithmetic: 2.65 us -> none  [the longest x1 1.34 us: block(): return (attention.astype(jnp.bfloat16), projected)]
    pallas_call x0 -> x1, Pallas kernels: none -> 1.36 us  [block(): pl.pallas_call(finish, out_shape=(jax.ShapeDtypeStruct((own, head_count *...]
where the time goes in v1:
time: 24.9 us; the launch traced here: 24.6 us
  Pallas kernels  23.4 us (94%)
  between operations  1.28 us (5%)
    pallas_call x1, Pallas kernels, block(): pl.pallas_call(functools.partial(fused, n, heads), out_shape=(jax.ShapeDt...  22 us
    pallas_call x1, Pallas kernels, block(): pl.pallas_call(finish, out_shape=(jax.ShapeDtypeStruct((own, head_count *...  1.36 us

profile of v1, /device:TPU:0, one launch (start us, length us, event | category | flops | bytes accessed | tf_op | source)
XLA Modules:
  0.0 24.6 jit_solution(7514444913034883345)
XLA Ops:
  1.3 22.0 %mla_block.1 = (f32[1,4096]{1,0:T(1,128)}, f32[4,896]{1,0:T(4,128)}) custom-call(s32[1]{0:T(128)S(6)} %copy.10.valid_hbm, s32[8]{0:T(128)} %qpos_hbm.1, bf16[1,32,576]{2,1,0:T(8,128)(2,1)} %query_hbm.1, bf16[6,96,256]{2,1,0:T(8,128)(2,1)} %bitcast.4, f32[9,256]{1,0:T(8,128)} %bitcast.5, bf16[32,512,128]{2,1,0:T(8,128)(2,1)} %up_hbm.1, bf16[4096,896]{1,0:T(8,128)(2,1)} %out_hbm.1), custom_call_target="tpu_custom_call" | custom-call | tf_op jit(solution)/shard_map/mla_block/pallas_call | solution.py:451
  23.3 1.4 %finish.1 = (bf16[1,4096]{1,0:T(2,128)(2,1)}, bf16[4,896]{1,0:T(4,128)(2,1)}) custom-call(f32[1,4096]{1,0:T(1,128)} %get-tuple-element.4.attn_ref, f32[4,896]{1,0:T(4,128)} %get-tuple-element.5.summed_ref, f32[896]{0:T(1024)} %scales_ref.1), custom_call_target="tpu_custom_call" | custom-call | tf_op jit(solution)/shard_map/finish/pallas_call | solution.py:514

commit v2 on v1

--- a/solution.py
+++ b/solution.py
@@ -150,8 +150,9 @@
     row, column = me // 2, lax.rem(me, 2)
     rows = n // 2
     head_count, width = q_all.shape[1:]
-    pieces, piece, keys = codes.shape
-    each = pieces // heads
+    blocks, block, keys = codes.shape
+    pairs = (blocks - 1) // 2
+    rest = pl.ds(2 * pairs, blocks - 2 * pairs)
     nope = mix.shape[0] * LANES
     vhead = up.shape[2]
     twin = head_count // 2
@@ -159,14 +160,17 @@
     lines = 2 * rows
 
     barrier = pltpu.get_barrier_semaphore()
-    for k in range(n - 1, 0, -1):
+    met = [1] + list(range(2, n, 2))
+    for k in met:
         later = flip(me, k)
 
         @pl.when(later > me)
         def _():
             pl.semaphore_signal(barrier, inc=1, device_id={"ctx": later}, device_id_type=MESH)
 
-    pl.semaphore_signal(barrier, inc=1, device_id={"head": other}, device_id_type=MESH)
+    @pl.when(hd == 0)
+    def _():
+        pl.semaphore_signal(barrier, inc=1, device_id={"head": other}, device_id_type=MESH)
 
     loads = [
         pltpu.make_async_copy(codes_hbm, codes, in_sem.at[0]),
@@ -178,9 +182,17 @@
     for copy in loads:
         copy.start()
 
-    pl.semaphore_wait(barrier, me + heads - 1)
-
-    for k in range(1, n):
+    ahead = row + column + hd
+
+    @pl.when(ahead > 0)
+    def _():
+        pl.semaphore_wait(barrier, ahead)
+
+    @pl.when(hd == 1)
+    def _():
+        pl.semaphore_signal(ready.at[0], inc=1, device_id={"head": other}, device_id_type=MESH)
+
+    for k in met:
         earlier = flip(me, k)
 
         @pl.when(earlier < me)
@@ -192,7 +204,10 @@
         def _():
             pl.semaphore_wait(ready.at[k], 1)
 
-    def remote(src, dst, ssem, rsem, **device):
+    def owner(p):
+        return int(p >= 1)
+
+    def remote(src, dst, ssem, rsem, when=None, **device):
         copy = pltpu.make_async_remote_copy(
             src_ref=src,
             dst_ref=dst,
@@ -201,36 +216,48 @@
             device_id=device,
             device_id_type=MESH,
         )
-        copy.start()
+        copy.start() if when is None else pl.when(when)(copy.start)
         return copy
+
+    queries = []
+    for k in range(1, rows):
+        peer = flip(me, 2 * k)
+        queries.append(remote(query_hbm.at[0], q_all.at[row], q_ssem.at[k], q_rsem.at[k], peer < me, ctx=peer))
 
     admit(1)
     partner = flip(me, 1)
     near = [
-        remote(
-            codes_hbm.at[hd * each + i],
-            near_codes.at[hd * each + i],
-            near_ssem.at[i],
-            near_rsem.at[i],
-            ctx=partner,
-        )
-        for i in range(each)
+        remote(valid_hbm, near_valid, near_ssem.at[0], near_rsem.at[0], ctx=partner),
+        remote(scales_hbm, near_scales, near_ssem.at[1], near_rsem.at[1], hd == 1, ctx=partner),
     ]
-    near.append(remote(scales_hbm, near_scales, near_ssem.at[each], near_rsem.at[each], ctx=partner))
-    near.append(remote(valid_hbm, near_valid, near_ssem.at[each + 1], near_rsem.at[each + 1], ctx=partner))
+    for p in range(pairs):
+        of = pl.ds(2 * p, 2)
+        near.append(
+            remote(
+                codes_hbm.at[of],
+                near_codes.at[of],
+                near_ssem.at[2 + p],
+                near_rsem.at[2 + p],
+                hd == owner(p),
+                ctx=partner,
+            )
+        )
+    last = remote(
+        codes_hbm.at[rest],
+        near_codes.at[rest],
+        near_ssem.at[2 + pairs],
+        near_rsem.at[2 + pairs],
+        ctx=partner,
+    )
 
     up_in = []
     for g in range(2):
         part_of = pl.ds(g * twin, twin)
         up_in.append(pltpu.make_async_copy(up_hbm.at[part_of], up.at[part_of], up_sem.at[g]))
         up_in[-1].start()
-
-    queries = []
     for k in range(1, rows):
         admit(2 * k)
-        queries.append(
-            remote(query_hbm.at[0], q_all.at[row], q_ssem.at[k], q_rsem.at[k], ctx=flip(me, 2 * k))
-        )
+        pl.when(flip(me, 2 * k) > me)(queries[k - 1].start)
 
     out_in = []
     half = outw.shape[0] // 2
@@ -238,47 +265,50 @@
         part_of = pl.ds(g * half, half)
         out_in.append(pltpu.make_async_copy(out_hbm.at[part_of], outw.at[part_of], out_sem.at[g]))
         out_in[-1].start()
-
-    block = width // scales.shape[0]
-
-    def scale_latent(source, factors, target):
-        unit = math.gcd(piece, block)
-        for p in range(pieces):
-            for r in range(0, piece, unit):
-                at = p * piece + r
-                b = at // block
-                target[at : at + unit, :] = (
-                    source[p, r : r + unit, :].astype(jnp.float32) * factors[b : b + 1, :]
-                ).astype(jnp.bfloat16)
+    def scale_latent(source, factors, target, of):
+        for b in of:
+            target[b * block : (b + 1) * block, :] = (
+                source[b].astype(jnp.float32) * factors[b : b + 1, :]
+            ).astype(jnp.bfloat16)
 
     for copy in loads:
         copy.wait()
-    scale_latent(codes, scales, latent)
+    scale_latent(codes, scales, latent, range(blocks))
 
     relayed = []
-    for i in range(each):
-        near[i].wait_recv()
+
+    def relay(ref, index, who):
+        pl.when(hd == who)(near[index].wait_recv)
         relayed.append(
-            remote(
-                near_codes.at[hd * each + i],
-                near_codes.at[hd * each + i],
-                half_ssem.at[i],
-                half_rsem.at[i],
-                head=other,
-            )
-        )
-    for copy in near[each:]:
-        copy.wait_recv()
+            remote(ref, ref, half_ssem.at[index], half_rsem.at[index], hd == who, head=other)
+        )
+
+    @pl.when(hd == 0)
+    def _():
+        pl.semaphore_wait(ready.at[0], 1)
+
+    relay(near_scales, 1, 1)
+    for p in range(pairs):
+        relay(near_codes.at[pl.ds(2 * p, 2)], 2 + p, owner(p))
     for copy in queries:
         copy.wait_recv()
-    for copy in relayed:
-        copy.wait_recv()
-    scale_latent(near_codes, near_scales, near_latent)
-
     softmax_scale = (QK_NOPE + ROPE) ** (-0.5)
     query = q_all[...].reshape(rows * head_count, width)
     own_logits = jnp.dot(query, latent[...], preferred_element_type=jnp.float32) * softmax_scale
-    near_logits = jnp.dot(query, near_latent[...], preferred_element_type=jnp.float32) * softmax_scale
+    pl.when(hd == 0)(relayed[0].wait_recv)
+    near[0].wait_recv()
+    near_logits = None
+    for p in list(range(pairs - 1)) + [pairs, pairs - 1]:
+        if p < pairs:
+            pl.when(hd != owner(p))(relayed[1 + p].wait_recv)
+        else:
+            last.wait_recv()
+        of = range(2 * p, min(2 * p + 2, blocks))
+        scale_latent(near_codes, near_scales, near_latent, of)
+        lanes = slice(of[0] * block, (of[-1] + 1) * block)
+        term = jnp.dot(query[:, lanes], near_latent[lanes, :], preferred_element_type=jnp.float32)
+        near_logits = term if near_logits is None else near_logits + term
+    near_logits = near_logits * softmax_scale
     slot = lax.broadcasted_iota(jnp.int32, (head_count, keys), 1)
     own_weights, near_weights = [], []
     for t in range(rows):
@@ -363,8 +393,6 @@
 
     shared = {}
     for k in range(n - 1, 0, -1):
-        if k % 2 and k > 1:
-            admit(k)
         shared[k] = remote(
             att_all.at[row, column],
             att_all.at[row, column],
@@ -372,8 +400,11 @@
             att_rsem.at[k],
             ctx=flip(me, k),
         )
-    for copy in near + queries + relayed + moved:
+    for copy in [near[0], last] + queries + moved:
         copy.wait_send()
+    for p in range(-1, pairs):
+        pl.when(hd == (owner(p) if p >= 0 else 1))(near[2 + p].wait_send)
+        pl.when(hd == (owner(p) if p >= 0 else 1))(relayed[1 + p].wait_send)
     for copy in out_in:
         copy.wait()
     columns = outw.shape[1]
@@ -436,9 +467,9 @@
     query, codes, scales, valid, qpos, up, outw, out_scales = args
     own, head_count, width = query.shape
     keys, blocks = scales.shape
-    split = 3 * heads
+    chunk = (blocks - 1) // 2 + 3
     fits = own == 1 and heads == 2 and n >= 4 and n & (n - 1) == 0 and head_count % n == 0
-    fits = fits and width % (split * 16) == 0
+    fits = fits and width % blocks == 0 and 2 * width // blocks % LANES == 0 and blocks > 2
     if not fits:
         return shards(*args)
     vhead = up.shape[2]
@@ -461,8 +492,8 @@
             pltpu.SMEM(qpos.shape, jnp.int32),
             pltpu.SMEM(valid.shape, jnp.int32),
             pltpu.VMEM((rows, head_count, width), jnp.bfloat16),
-            pltpu.VMEM((split, width // split, keys), jnp.bfloat16),
-            pltpu.VMEM((split, width // split, keys), jnp.bfloat16),
+            pltpu.VMEM((blocks, width // blocks, keys), jnp.bfloat16),
+            pltpu.VMEM((blocks, width // blocks, keys), jnp.bfloat16),
             pltpu.VMEM((blocks, keys), jnp.float32),
             pltpu.VMEM((blocks, keys), jnp.float32),
             pltpu.VMEM(up.shape, jnp.bfloat16),
@@ -485,10 +516,10 @@
             dma((2,)),
             dma((rows,)),
             dma((rows,)),
-            dma((split // heads + 2,)),
-            dma((split // heads + 2,)),
-            dma((split // heads,)),
-            dma((split // heads,)),
+            dma((chunk,)),
+            dma((chunk,)),
+            dma((chunk,)),
+            dma((chunk,)),
             dma((rows,)),
             dma((rows,)),
             dma((rows,)),
@@ -499,17 +530,22 @@
             dma((1,)),
         ],
         compiler_params=pltpu.CompilerParams(
-            collective_id=0, has_side_effects=True
+            collective_id=0, has_side_effects=True, vmem_limit_bytes=32 * 1024 * 1024
         ),
         name="mla_block",
     )(
         valid,
-        qpos,
-        query,
-        codes.T.reshape(split, width // split, keys),
-        scales.T,
-        up,
-        outw,
+        *(
+            pltpu.with_memory_space_constraint(operand, pltpu.HBM)
+            for operand in (
+                qpos,
+                query,
+                codes.T.reshape(blocks, width // blocks, keys),
+                scales.T,
+                up,
+                outw,
+            )
+        ),
     )
     return pl.pallas_call(
         finish,
@@ -519,6 +555,7 @@
         ),
         in_specs=[vmem] * 3,
         out_specs=(vmem, vmem),
+        compiler_params=pltpu.CompilerParams(vmem_limit_bytes=1024 * 1024),
         name="finish",
     )(attention, summed, out_scales)
 

time: 24.9 us -> 23.8 us (0.956)
  Pallas kernels: 23.4 us -> 22.3 us
    pallas_call x1, Pallas kernels: 1.36 us -> 0.62 us  [block(): pl.pallas_call(finish, out_shape=(jax.ShapeDtypeStruct((own, head_count *...]
    pallas_call x1, Pallas kernels: 22 us -> 21.7 us  [block(): pl.pallas_call(functools.partial(fused, n, heads), out_shape=(jax.ShapeDt...]
where the time goes in v2:
time: 23.8 us; the launch traced here: 23.6 us
  Pallas kernels  22.3 us (94%)
  between operations  1.31 us (6%)
    pallas_call x1, Pallas kernels, block(): pl.pallas_call(functools.partial(fused, n, heads), out_shape=(jax.ShapeDt...  21.7 us
    pallas_call x1, Pallas kernels, block(): pl.pallas_call(finish, out_shape=(jax.ShapeDtypeStruct((own, head_count *...  0.62 us

profile of v2, /device:TPU:0, one launch (start us, length us, event | category | flops | bytes accessed | tf_op | source)
XLA Modules:
  0.0 23.6 jit_solution(9858313452839651196)
XLA Ops:
  0.6 0.0 copy-start
  1.3 21.7 %mla_block.1 = (f32[1,4096]{1,0:T(1,128)S(1)}, f32[4,896]{1,0:T(4,128)S(1)}) custom-call(s32[1]{0:T(128)S(6)} %copy.10.valid_hbm, s32[8]{0:T(128)} %qpos_hbm.1, bf16[1,32,576]{2,1,0:T(8,128)(2,1)} %query_hbm.1, bf16[9,64,256]{2,1,0:T(8,128)(2,1)} %bitcast.4, f32[9,256]{1,0:T(8,128)} %bitcast.5, bf16[32,512,128]{2,1,0:T(8,128)(2,1)} %up_hbm.1, ...), custom_call_target="tpu_custom_call" | custom-call | tf_op jit(solution)/shard_map/mla_block/pallas_call | solution.py:482
  23.0 0.0 copy-done
  23.0 0.6 %finish.1 = (bf16[1,4096]{1,0:T(2,128)(2,1)}, bf16[4,896]{1,0:T(4,128)(2,1)}) custom-call(f32[1,4096]{1,0:T(1,128)S(1)} %get-tuple-element.4.attn_ref, f32[4,896]{1,0:T(4,128)S(1)} %get-tuple-element.5.summed_ref, f32[896]{0:T(1024)S(1)} %copy-done), custom_call_target="tpu_custom_call" | custom-call | tf_op jit(solution)/shard_map/finish/pallas_call | solution.py:550
Async XLA Ops:
  0.6 22.4 %copy-start = (f32[896]{0:T(1024)S(1)}, f32[896]{0:T(1024)}, u32[]{:S(2)}) copy-start(f32[896]{0:T(1024)} %scales_ref.1) | copy-start | bytes 10756
